TPU v7x, 8 devices: a whole 2x2x1 slice. The times are simulated.
8 devices in a mesh: data: 8 (over z, y, x, core).
Axes of the slice: x: 2, y: 2, z: 1, core: 2. Of those that a mesh axis runs over, the one named last changes fastest.
Arguments:
- tokens: bfloat16 [65536, 256], P('data')
- out_grad: bfloat16 [65536, 256], P('data')
- w_up: bfloat16 [2, 256, 1024], replicated
- w_down: bfloat16 [2, 1024, 256], replicated
- a_up_old: float32 [2, 256, 256], replicated
- s_up_old: float32 [2, 1024, 1024], replicated
- a_down_old: float32 [2, 1024, 1024], replicated
- s_down_old: float32 [2, 256, 256], replicated
- a_up_inv: float32 [2, 256, 256], replicated
- s_up_inv: float32 [2, 1024, 1024], replicated
- a_down_inv: float32 [2, 1024, 1024], replicated
- s_down_inv: float32 [2, 256, 256], replicated
- factor_decay: float32 [], replicated
Outputs:
- output 1: float32 [2, 256, 1024], replicated
- output 2: float32 [2, 1024, 256], replicated
- output 3: float32 [2, 256, 256], replicated
- output 4: float32 [2, 1024, 1024], replicated
- output 5: float32 [2, 1024, 1024], replicated
- output 6: float32 [2, 256, 256], replicated
All inputs are finite; a program needn't handle non-finite values.
Results may differ from a plain program's by a relative error of at most 0.00171.
Values are sent between devices in bfloat16 or wider.
A program may use at most 1 GiB of HBM per device.

v0:
```python
import jax
import jax.numpy as jnp
from jax import lax
from jax.sharding import PartitionSpec as P, NamedSharding


def gelu_fn(pre_act):
    return jax.nn.gelu(pre_act, approximate=True)


def cross_sum(left, right):
    return jnp.einsum("ti,tj->ij", left, right, preferred_element_type=jnp.float32)


def stacked_sums(left_list, right_list, batch_total):
    return jnp.stack([cross_sum(left, right) for left, right in zip(left_list, right_list)]) / batch_total


def precise_chain(left, middle, right):
    inner_prod = jnp.einsum("bij,bjk->bik", left, middle, precision=lax.Precision.HIGHEST,
                            preferred_element_type=jnp.float32)
    return jnp.einsum("bij,bjk->bik", inner_prod, right, precision=lax.Precision.HIGHEST,
                      preferred_element_type=jnp.float32)


def forward_backward(tok_rows, grad_rows, w_up, w_down):
    block_count = w_up.shape[0]
    layer_ins = []
    pre_ups = []
    hiddens = []
    layer_in = tok_rows
    for block_idx in range(block_count):
        pre_up = jnp.dot(layer_in, w_up[block_idx], preferred_element_type=jnp.float32).astype(jnp.bfloat16)
        hidden = gelu_fn(pre_up.astype(jnp.float32)).astype(jnp.bfloat16)
        layer_ins.append(layer_in)
        pre_ups.append(pre_up)
        hiddens.append(hidden)
        if block_idx + 1 < block_count:
            layer_in = jnp.dot(hidden, w_down[block_idx], preferred_element_type=jnp.float32).astype(jnp.bfloat16)
    grad_ups = [None] * block_count
    grad_downs = [None] * block_count
    grad_down = grad_rows
    for block_idx in reversed(range(block_count)):
        grad_downs[block_idx] = grad_down
        d_hidden = jnp.einsum("tj,ij->ti", grad_down, w_down[block_idx],
                              preferred_element_type=jnp.float32).astype(jnp.bfloat16)
        gelu_back = jax.vjp(gelu_fn, pre_ups[block_idx].astype(jnp.float32))[1]
        grad_up = gelu_back(d_hidden.astype(jnp.float32))[0].astype(jnp.bfloat16)
        grad_ups[block_idx] = grad_up
        if block_idx > 0:
            grad_down = jnp.einsum("tj,ij->ti", grad_up, w_up[block_idx],
                                   preferred_element_type=jnp.float32).astype(jnp.bfloat16)
    return layer_ins, hiddens, grad_ups, grad_downs


def update_outputs(dw_up, dw_down, fresh_factors, old_factors, inverses, factor_decay):
    new_factors = tuple(factor_decay * old_part + (1.0 - factor_decay) * new_part
                        for old_part, new_part in zip(old_factors, fresh_factors))
    precond_up = precise_chain(inverses[0], dw_up, inverses[1])
    precond_down = precise_chain(inverses[2], dw_down, inverses[3])
    return (precond_up, precond_down) + new_factors


def solution(mesh):
    axis_size = mesh.shape["data"]

    def local_step(tok_rows, grad_rows, w_up, w_down, a_up_old, s_up_old, a_down_old, s_down_old,
                   a_up_inv, s_up_inv, a_down_inv, s_down_inv, factor_decay):
        batch_total = tok_rows.shape[0] * axis_size
        layer_ins, hiddens, grad_ups, grad_downs = forward_backward(tok_rows, grad_rows, w_up, w_down)
        local_parts = (stacked_sums(layer_ins, grad_ups, batch_total),
                       stacked_sums(hiddens, grad_downs, batch_total),
                       stacked_sums(layer_ins, layer_ins, batch_total),
                       stacked_sums(grad_ups, grad_ups, batch_total),
                       stacked_sums(hiddens, hiddens, batch_total),
                       stacked_sums(grad_downs, grad_downs, batch_total))
        totals = [lax.psum(part, "data") for part in local_parts]
        return update_outputs(totals[0], totals[1], tuple(totals[2:]),
                              (a_up_old, s_up_old, a_down_old, s_down_old),
                              (a_up_inv, s_up_inv, a_down_inv, s_down_inv), factor_decay)

    batch_spec = P("data", None)
    replicated = P()
    return jax.shard_map(local_step, mesh=mesh, in_specs=(batch_spec, batch_spec) + (replicated,) * 11,
                         out_specs=(replicated,) * 6, check_vma=False)
```

profile of v0, /device:TPU:0, one launch (start us, length us, event | category | flops | bytes accessed | tf_op | source)
XLA Modules:
  0.0 614.5 jit_solution(6054718594851495256)
XLA Ops:
  7.2 5.5 convolution_bitcast_fusion.11
  12.7 15.3 %fusion.13 = (bf16[8192,1024]{1,0:T(8,128)(2,1)S(1)}, bf16[8192,1024]{1,0:T(8,128)(2,1)}) fusion(bf16[8192,256]{1,0:T(8,128)(2,1)} %param.13, bf16[2,256,1024]{2,1,0:T(8,128)(2,1)} %param.15), kind=kOutput, calls=%fused_computation.25 | convolution fusion | flops 4387241984 | bytes 38273024 | tf_op jit(solution)/shard_map/dot_general | solution.py:33
  28.0 19.2 %convolution_bitcast_fusion.1 = f32[1,1024,1024]{2,1,0:T(8,128)} fusion(bf16[8192,1024]{1,0:T(8,128)(2,1)S(1)} %get-tuple-element.12), kind=kOutput, calls=%fused_computation.43 | convolution fusion | flops 17179869184 | bytes 20971520 | tf_op jit(solution)/shard_map/ti,tj->ij/dot_general | solution.py:12
  47.2 6.2 %convolution_convert_fusion.3 = bf16[8192,256]{1,0:T(8,128)(2,1)S(1)} fusion(bf16[8192,1024]{1,0:T(8,128)(2,1)S(1)} %get-tuple-element.12, bf16[2,1024,256]{2,1,0:T(8,128)(2,1)} %param.16), kind=kOutput, calls=%fused_computation.37 | convolution fusion | flops 4297064448 | bytes 21495808 | tf_op jit(solution)/shard_map/dot_general | solution.py:39
  57.4 10.3 %convolution_convert_fusion = bf16[8192,1024]{1,0:T(8,128)(2,1)} fusion(bf16[8192,256]{1,0:T(8,128)(2,1)} %copy-done.2, bf16[2,256,1024]{2,1,0:T(8,128)(2,1)S(1)} %copy-done.18), kind=kOutput, calls=%fused_computation.34 | convolution fusion | flops 4303355904 | bytes 21495808 | tf_op jit(solution)/shard_map/dot_general | solution.py:33
  67.8 5.6 convolution_bitcast_fusion.8
  73.4 17.5 %convolution_bitcast_fusion.5 = f32[1,1024,256]{2,1,0:T(8,128)} fusion(bf16[8192,256]{1,0:T(8,128)(2,1)} %param.14, bf16[8192,1024]{1,0:T(8,128)(2,1)} %convolution_convert_fusion), kind=kOutput, calls=%fused_computation.49 | convolution fusion | flops 4378853376 | bytes 22020096 | tf_op jit(solution)/shard_map/ti,tj->ij/dot_general | solution.py:12
  90.9 43.6 %convolution_bitcast_fusion = f32[1,1024,1024]{2,1,0:T(8,128)} fusion(bf16[8192,1024]{1,0:T(8,128)(2,1)S(1)} %bitcast.80), kind=kOutput, calls=%fused_computation.42 | convolution fusion | flops 17263755264 | bytes 20971520 | tf_op jit(solution)/shard_map/ti,tj->ij/dot_general | solution.py:12
  134.4 26.5 %fusion.4 = bf16[8192,1024]{1,0:T(8,128)(2,1)} fusion(bf16[8192,1024]{1,0:T(8,128)(2,1)S(1)} %bitcast.80, bf16[8192,256]{1,0:T(8,128)(2,1)S(1)} %copy-done.3, bf16[2,1024,256]{2,1,0:T(8,128)(2,1)S(1)} %copy-done.19), kind=kOutput, calls=%fused_computation.16 | convolution fusion | flops 4487905280 | bytes 38273024 | tf_op jit(solution)/shard_map/tj,ij->ti/dot_general | solution.py:45
  160.9 11.7 %convolution_bitcast_fusion.4 = f32[1,256,1024]{1,2,0:T(8,128)S(1)} fusion(bf16[8192,256]{1,0:T(8,128)(2,1)} %copy-done.2, bf16[8192,1024]{1,0:T(8,128)(2,1)} %fusion.4), kind=kOutput, calls=%fused_computation.48 | convolution fusion | flops 4294967296 | bytes 22020096 | tf_op jit(solution)/shard_map/ti,tj->ij/dot_general | solution.py:12
  172.6 10.4 %convolution_convert_fusion.2 = bf16[8192,256]{1,0:T(8,128)(2,1)S(1)} fusion(bf16[8192,1024]{1,0:T(8,128)(2,1)} %fusion.4, bf16[2,256,1024]{2,1,0:T(8,128)(2,1)S(1)} %copy-done.18), kind=kOutput, calls=%fused_computation.36 | convolution fusion | flops 4297064448 | bytes 21495808 | tf_op jit(solution)/shard_map/tj,ij->ti/dot_general | solution.py:51
  183.0 26.1 %convolution_bitcast_fusion.2 = f32[1,1024,1024]{2,1,0:T(8,128)} fusion(bf16[8192,1024]{1,0:T(8,128)(2,1)} %fusion.4), kind=kOutput, calls=%fused_computation.44 | convolution fusion | flops 17179869184 | bytes 20971520 | tf_op jit(solution)/shard_map/ti,tj->ij/dot_general | solution.py:12
  209.1 8.4 %convolution_bitcast_fusion.6 = f32[1,1024,256]{2,1,0:T(8,128)S(1)} fusion(bf16[8192,1024]{1,0:T(8,128)(2,1)} %copy-done.4, bf16[8192,256]{1,0:T(8,128)(2,1)S(1)} %convolution_convert_fusion.2), kind=kOutput, calls=%fused_computation.50 | convolution fusion | flops 4294967296 | bytes 22020096 | tf_op jit(solution)/shard_map/ti,tj->ij/dot_general | solution.py:12
  218.8 28.4 %fusion.7 = bf16[8192,1024]{1,0:T(8,128)(2,1)} fusion(bf16[8192,1024]{1,0:T(8,128)(2,1)} %get-tuple-element.13, bf16[8192,256]{1,0:T(8,128)(2,1)S(1)} %convolution_convert_fusion.2, bf16[2,1024,256]{2,1,0:T(8,128)(2,1)S(1)} %copy-done.20), kind=kOutput, calls=%fused_computation.19 | convolution fusion | flops 4487905280 | bytes 38273024 | tf_op jit(solution)/shard_map/tj,ij->ti/dot_general | solution.py:45
  247.3 8.3 %convolution_bitcast_fusion.7 = f32[1,256,1024]{1,2,0:T(8,128)S(1)} fusion(bf16[8192,1024]{1,0:T(8,128)(2,1)} %fusion.7, bf16[8192,256]{1,0:T(8,128)(2,1)S(1)} %copy-done.1), kind=kOutput, calls=%fused_computation.51 | convolution fusion | flops 4294967296 | bytes 22020096 | tf_op jit(solution)/shard_map/ti,tj->ij/dot_general | solution.py:12
  257.8 19.4 %convolution_bitcast_fusion.3 = f32[1,1024,1024]{2,1,0:T(8,128)} fusion(bf16[8192,1024]{1,0:T(8,128)(2,1)S(1)} %copy-done.5), kind=kOutput, calls=%fused_computation.45 | convolution fusion | flops 17179869184 | bytes 20971520 | tf_op jit(solution)/shard_map/ti,tj->ij/dot_general | solution.py:12
  278.1 9.4 %maximum_multiply_fusion.1 = f32[2,1024,1024]{2,1,0:T(8,128)} fusion(f32[1,1024,1024]{2,1,0:T(8,128)} %convolution_bitcast_fusion, f32[1,1024,1024]{2,1,0:T(8,128)} %convolution_bitcast_fusion.1), kind=kLoop, calls=%fused_computation.39 | loop fusion | flops 4194304 | bytes 16777216 | tf_op jit(solution)/shard_map/div | solution.py:16
  289.7 4.4 maximum_multiply_fusion
  296.3 264.0 %all-reduce.3.cloned.1.call-done = (f32[2,256,1024]{1,2,0:T(8,128)}, f32[2,1024,256]{2,1,0:T(8,128)}, f32[2,256,256]{2,1,0:T(8,128)}, f32[2,1024,1024]{2,1,0:T(8...) async-done(((f32[2,256,1024]{1,2,0:T(8,128)}, f32[2,1024,256]{2,1,0:T(8,128)}, f32[2,256,256]{2,1,0:T(8,128)}, f32[2,1024,1024]{2,1,0:T(8,128)}, ...) | async-done | bytes 22020112 | tf_op jit(solution)/shard_map/psum | solution.py:77
  560.3 3.7 fusion.36
  564.1 10.8 %fusion.37 = f32[2,256,1024]{2,1,0:T(8,128)} fusion(f32[2,1024,256]{1,2,0:T(8,128)S(1)} %fusion.36, f32[2,1024,1024]{2,1,0:T(8,128)} %param.22), kind=kOutput, calls=%fused_computation.73 | convolution fusion | flops 6442450944 | bytes 12582912 | tf_op jit(solution)/shard_map/bij,bjk->bik/dot_general | solution.py:22
  574.9 9.2 %fusion.38 = f32[2,256,1024]{1,2,0:T(8,128)S(1)} fusion(f32[2,1024,256]{2,1,0:T(8,128)S(1)} %copy-done.8, f32[2,1024,1024]{2,1,0:T(8,128)} %param.23), kind=kOutput, calls=%fused_computation.74 | convolution fusion | flops 6442450944 | bytes 12582912 | tf_op jit(solution)/shard_map/bij,bjk->bik/dot_general | solution.py:20
  584.0 3.3 fusion.39
  588.4 18.8 %multiply_add_fusion = (f32[2,1024,1024]{2,1,0:T(8,128)}, f32[2,1024,1024]{2,1,0:T(8,128)}) fusion(f32[2,1024,1024]{2,1,0:T(8,128)} %get-tuple-element.10, f32[2,1024,1024]{2,1,0:T(8,128)} %param.19, f32[]{:T(128)S(6)} %sub.14, f32[]{:T(128)S(6)} %copy.27, f32[2,1024,1024]{2,1,0:T(8,128)} %get-tuple-element.9, f32[2,1024,1024]{2,1,0:T(8,128)} %param.18), kind=kLoop, calls=%fused_computation.40 | loop fusion | flops 12582912 | bytes 50331656 | tf_op jit(solution)/shard_map/add | solution.py:57
  (60 shorter events, 13.4 us)
Async XLA Ops:
  7.2 553.1 %copy-start = (f32[2,256,256]{2,1,0:T(8,128)S(1)}, f32[2,256,256]{2,1,0:T(8,128)}, u32[]{:S(2)}) copy-start(f32[2,256,256]{2,1,0:T(8,128)} %param.21) | copy-start | bytes 1572868
  7.2 553.1 %all-reduce.3.cloned.1.call-start = ((), (), s32[]{:S(2)}) async-start(), calls=%async_computation | async-start | bytes 44040192 | tf_op jit(solution)/shard_map/psum | solution.py:77
  28.0 19.2 %copy-start.4 = (bf16[8192,1024]{1,0:T(8,128)(2,1)}, bf16[8192,1024]{1,0:T(8,128)(2,1)S(1)}, u32[]{:S(2)}) copy-start(bf16[8192,1024]{1,0:T(8,128)(2,1)S(1)} %get-tuple-element.12) | copy-start | bytes 50331652
  47.2 10.2 %copy-start.18 = (bf16[2,256,1024]{2,1,0:T(8,128)(2,1)S(1)}, bf16[2,256,1024]{2,1,0:T(8,128)(2,1)}, u32[]{:S(2)}) copy-start(bf16[2,256,1024]{2,1,0:T(8,128)(2,1)} %param.15) | copy-start | bytes 3145732
  67.8 23.1 %slice-start = ((s8[16777216]{0:T(1024)(128)(4,1)}), s8[4194304]{0:T(1024)(128)(4,1)S(1)}, s32[]{:S(2)}) async-start(s8[16777216]{0:T(1024)(128)(4,1)} %bitcast.79), calls=%async_computation.1 | async-start | bytes 8388608
  73.3 17.5 %slice-start.1 = ((s8[16777216]{0:T(1024)(128)(4,1)}), s8[4194304]{0:T(1024)(128)(4,1)S(1)}, s32[]{:S(2)}) async-start(s8[16777216]{0:T(1024)(128)(4,1)} %bitcast.79), calls=%async_computation.2 | async-start | bytes 8388608
  73.3 17.5 %slice-start.2 = ((s8[16777216]{0:T(1024)(128)(4,1)}), s8[4194304]{0:T(1024)(128)(4,1)S(1)}, s32[]{:S(2)}) async-start(s8[16777216]{0:T(1024)(128)(4,1)} %bitcast.79), calls=%async_computation.3 | async-start | bytes 8388608
  73.4 17.5 %slice-start.3 = ((s8[16777216]{0:T(1024)(128)(4,1)}), s8[4194304]{0:T(1024)(128)(4,1)S(1)}, s32[]{:S(2)}) async-start(s8[16777216]{0:T(1024)(128)(4,1)} %bitcast.79), calls=%async_computation.4 | async-start | bytes 8388608
  90.9 43.6 %copy-start.3 = (bf16[8192,256]{1,0:T(8,128)(2,1)S(1)}, bf16[8192,256]{1,0:T(8,128)(2,1)}, u32[]{:S(2)}) copy-start(bf16[8192,256]{1,0:T(8,128)(2,1)} %param.14) | copy-start | bytes 12582916
  90.9 43.6 %copy-start.19 = (bf16[2,1024,256]{2,1,0:T(8,128)(2,1)S(1)}, bf16[2,1024,256]{2,1,0:T(8,128)(2,1)}, u32[]{:S(2)}) copy-start(bf16[2,1024,256]{2,1,0:T(8,128)(2,1)} %param.16) | copy-start | bytes 3145732
  218.8 28.4 %copy-start.1 = (bf16[8192,256]{1,0:T(8,128)(2,1)S(1)}, bf16[8192,256]{1,0:T(8,128)(2,1)}, u32[]{:S(2)}) copy-start(bf16[8192,256]{1,0:T(8,128)(2,1)} %param.13) | copy-start | bytes 12582916
  247.2 10.5 %copy-start.5 = (bf16[8192,1024]{1,0:T(8,128)(2,1)S(1)}, bf16[8192,1024]{1,0:T(8,128)(2,1)}, u32[]{:S(2)}) copy-start(bf16[8192,1024]{1,0:T(8,128)(2,1)} %fusion.7) | copy-start | bytes 50331652
  257.8 19.4 %copy-start.9 = (f32[1,256,256]{2,1,0:T(8,128)S(1)}, f32[1,256,256]{2,1,0:T(8,128)}, u32[]{:S(2)}) copy-start(f32[1,256,256]{2,1,0:T(8,128)} %convolution_bitcast_fusion.11) | copy-start | bytes 786436
  257.8 19.4 %copy-start.11 = (f32[1,256,256]{2,1,0:T(8,128)S(1)}, f32[1,256,256]{2,1,0:T(8,128)}, u32[]{:S(2)}) copy-start(f32[1,256,256]{2,1,0:T(8,128)} %convolution_bitcast_fusion.10) | copy-start | bytes 786436
  277.2 10.2 %copy-start.10 = (f32[1,256,256]{2,1,0:T(8,128)S(1)}, f32[1,256,256]{2,1,0:T(8,128)}, u32[]{:S(2)}) copy-start(f32[1,256,256]{2,1,0:T(8,128)} %convolution_bitcast_fusion.8) | copy-start | bytes 786436
  277.2 11.0 %copy-start.12 = (f32[1,1024,256]{2,1,0:T(8,128)S(1)}, f32[1,1024,256]{2,1,0:T(8,128)}, u32[]{:S(2)}) copy-start(f32[1,1024,256]{2,1,0:T(8,128)} %convolution_bitcast_fusion.5) | copy-start | bytes 3145732
  277.2 12.5 %copy-start.6 = (f32[1,1024,1024]{2,1,0:T(8,128)S(1)}, f32[1,1024,1024]{2,1,0:T(8,128)}, u32[]{:S(2)}) copy-start(f32[1,1024,1024]{2,1,0:T(8,128)} %convolution_bitcast_fusion.2) | copy-start | bytes 12582916
  277.2 12.5 %copy-start.7 = (f32[1,1024,1024]{2,1,0:T(8,128)S(1)}, f32[1,1024,1024]{2,1,0:T(8,128)}, u32[]{:S(2)}) copy-start(f32[1,1024,1024]{2,1,0:T(8,128)} %convolution_bitcast_fusion.3) | copy-start | bytes 12582916
  295.6 288.5 %copy-start.13 = (f32[2,256,256]{2,1,0:T(8,128)S(1)}, f32[2,256,256]{2,1,0:T(8,128)}, u32[]{:S(2)}) copy-start(f32[2,256,256]{2,1,0:T(8,128)} %param.24) | copy-start | bytes 1572868
  560.3 14.6 %copy-start.8 = (f32[2,1024,256]{2,1,0:T(8,128)S(1)}, f32[2,1024,256]{2,1,0:T(8,128)}, u32[]{:S(2)}) copy-start(f32[2,1024,256]{2,1,0:T(8,128)} %get-tuple-element.7) | copy-start | bytes 6291460
  560.3 27.0 %copy-start.14 = (f32[2,256,256]{2,1,0:T(8,128)S(1)}, f32[2,256,256]{2,1,0:T(8,128)}, u32[]{:S(2)}) copy-start(f32[2,256,256]{2,1,0:T(8,128)} %param.20) | copy-start | bytes 1572868
  560.3 27.0 %copy-start.15 = (f32[2,256,256]{2,1,0:T(8,128)S(1)}, f32[2,256,256]{2,1,0:T(8,128)}, u32[]{:S(2)}) copy-start(f32[2,256,256]{2,1,0:T(8,128)} %param.17) | copy-start | bytes 1572868
  560.3 27.0 %copy-start.16 = (f32[2,256,256]{2,1,0:T(8,128)S(1)}, f32[2,256,256]{2,1,0:T(8,128)}, u32[]{:S(2)}) copy-start(f32[2,256,256]{2,1,0:T(8,128)} %get-tuple-element.8) | copy-start | bytes 1572868
  560.3 27.0 %copy-start.17 = (f32[2,256,256]{2,1,0:T(8,128)S(1)}, f32[2,256,256]{2,1,0:T(8,128)}, u32[]{:S(2)}) copy-start(f32[2,256,256]{2,1,0:T(8,128)} %get-tuple-element.11) | copy-start | bytes 1572868
  (2 other events, 11.7 us)
Sparse Core Ops, SparseCore 0:
  295.7 264.5 all-reduce.2
where the time goes:
time: 623 us; the launch traced here: 614 us
  matrix products  293 us (47%)
  waiting for transfers between devices  264 us (42%)
  other arithmetic  38.2 us (6%)
  between operations  15.4 us (2%)
    psum x1, waiting for transfers between devices, local_step(): totals = [lax.psum(part, 'data') for part in local_parts]  264 us
    dot_general x12, matrix products, cross_sum(): jnp.einsum('ti,tj->ij', left, right, preferred_element_type=jnp.float32)  168 us
    dot_general x2, matrix products, forward_backward(): jnp.einsum('tj,ij->ti', grad_down, w_down[block_idx], preferred_element_t...  54.9 us
    dot_general x2, matrix products, forward_backward(): jnp.dot(layer_in, w_up[block_idx], preferred_element_type=jnp.float32)  25.6 us
    add x2, other arithmetic, update_outputs(): factor_decay * old_part + (1.0 - factor_decay) * new_part  19.9 us
    div x6, other arithmetic, stacked_sums(): jnp.stack([cross_sum(left, right) for left, right in zip(left_list, right...  18.3 us
    dot_general x2, matrix products, precise_chain(): jnp.einsum('bij,bjk->bik', inner_prod, right, precision=lax.Precision.HIG...  14.1 us
    dot_general x2, matrix products, precise_chain(): jnp.einsum('bij,bjk->bik', left, middle, precision=lax.Precision.HIGHEST,...  12.9 us
  transfers between devices with their start and end apart: 1, of which 1 were waited for; matrix products, arithmetic and copies ran while one was open for 0% of the time, Pallas kernels for 0%

commit v1 on v0

v1 whole, which is shorter than its diff:
```python
import functools

import jax
import jax.numpy as jnp
from jax import lax
from jax.experimental import pallas as pl
from jax.experimental.pallas import tpu as pltpu
from jax.sharding import PartitionSpec as P

F32 = jnp.float32
BF16 = jnp.bfloat16
MESH = pl.DeviceIdType.MESH
HIGHEST = lax.Precision.HIGHEST

D = 256
FF = 1024
TILE = 512
C0 = 0.7978845608028654
C1 = C0 * 0.044715

AU0, SD1, AD0, AD1, AU1, SU1, DU1, DD1, SU0, DU0, DD0, SD0 = 0, 1, 2, 12, 22, 23, 33, 37, 41, 51, 55, 59
BLOCKS = 60
AU = (AU0, AU1)
SD = (SD0, SD1)
AD = (AD0, AD1)
SU = (SU0, SU1)
DU = (DU0, DU1)
DD = (DD0, DD1)
UPPER = [(i, j) for j in range(4) for i in range(j + 1)]

UNITS = [(0, 6, 0), (6, 6, 6), (12, 10, 12), (22, 11, 22), (33, 8, 33), (41, 10, 12), (51, 9, 22)]
POOL = 41
ALL = tuple(range(len(UNITS)))


def upper_index(i, j):
    return j * (j + 1) // 2 + i


def block_kinds():
    kinds = {}
    for b in range(2):
        for i, j in UPPER:
            kinds[AD[b] + upper_index(i, j)] = ("big", 0, b, i, j)
            kinds[SU[b] + upper_index(i, j)] = ("big", 1, b, i, j)
        kinds[AU[b]] = ("small", 0, b, 0, 0)
        kinds[SD[b]] = ("small", 1, b, 0, 0)
    return kinds


KINDS = block_kinds()


def nn(a, b, precision=None):
    return lax.dot_general(a, b, (((1,), (0,)), ((), ())), preferred_element_type=F32, precision=precision)


def nt(a, b):
    return lax.dot_general(a, b, (((1,), (1,)), ((), ())), preferred_element_type=F32)


def half_gelu(z):
    sq = z * z
    return sq, jnp.tanh(z * (C1 * sq + C0)) * 0.5 + 0.5


def main_kernel(rows, batch_total,
                tok_hbm, grad_hbm, wup, wdn, rho_ref, a_up_old, s_up_old, a_down_old, s_down_old, s_up_inv, a_down_inv,
                out, tok, grad, wup_t, wdn_t, u1_t, e1_t, h_t, g_t, acc, big_old, small_old, inv,
                r0, r1, r2, tok_sem, grad_sem, old_sem, inv_sem, out_sem, send_sem, recv_sem, sent_sem):
    tiles = rows // TILE
    me = lax.axis_index("data")
    core = lax.rem(me, 2)
    xpos = lax.rem(me // 2, 2)
    ypos = me // 4
    core_peer = me + 1 - 2 * core
    x_peer = me + 2 - 4 * xpos
    y_peer = me + 4 - 8 * ypos

    barrier = pltpu.get_barrier_semaphore()
    for peer in (core_peer, x_peer, y_peer):
        pl.semaphore_signal(barrier, inc=1, device_id=(peer,), device_id_type=MESH)

    def tok_copy(i):
        ds = pl.ds(i * TILE, TILE)
        return pltpu.make_async_copy(tok_hbm.at[ds, :], tok.at[ds, :], tok_sem.at[i])

    def grad_copy(i):
        ds = pl.ds(i * TILE, TILE)
        return pltpu.make_async_copy(grad_hbm.at[ds, :], grad.at[ds, :], grad_sem.at[i])

    for i in range(tiles):
        tok_copy(i).start()
        grad_copy(i).start()

    half = core * 128
    a_half = half + xpos * 32
    b_half = half + 64 + ypos * 32
    own_a = a_half + ypos * 16
    own_b = b_half + xpos * 16
    own = (own_a, own_b)

    for m, old in enumerate((a_down_old, s_up_old)):
        for b in range(2):
            for i in range(4):
                for p in range(2):
                    pltpu.make_async_copy(old.at[b, pl.ds(i * 256 + own[p], 16), :],
                                          big_old.at[m, b, i, pl.ds(p * 16, 16), :], old_sem.at[0]).start()
    for m, old in enumerate((a_up_old, s_down_old)):
        for b in range(2):
            for p in range(2):
                pltpu.make_async_copy(old.at[b, pl.ds(own[p], 16), :],
                                      small_old.at[m, b, pl.ds(p * 16, 16), :], old_sem.at[1]).start()

    def inv_copies(b):
        return (pltpu.make_async_copy(s_up_inv.at[b], inv.at[0], inv_sem.at[0]),
                pltpu.make_async_copy(a_down_inv.at[b], inv.at[1], inv_sem.at[1]))

    for copy in inv_copies(1):
        copy.start()

    for b in range(2):
        wup_t[b] = wup[b].T
    wdn_t[...] = wdn[0].T
    acc[...] = jnp.zeros_like(acc)

    pltpu.make_async_copy(big_old, big_old, old_sem.at[0]).wait()
    pltpu.make_async_copy(small_old, small_old, old_sem.at[1]).wait()
    pl.semaphore_wait(barrier, 3)

    def remote(u, slot, src, dst, peer):
        return pltpu.make_async_remote_copy(src_ref=src, dst_ref=dst, send_sem=send_sem.at[u, slot],
                                            recv_sem=recv_sem.at[u, slot], device_id=(peer,), device_id_type=MESH)

    def exchange(u, stage):
        b0, n, p0 = UNITS[u]
        blk = pl.ds(b0, n)
        pool = pl.ds(p0, n)

        def at(row, count):
            return acc.at[blk, pl.ds(pl.multiple_of(row, 16), count), :]

        if stage == 0:
            return [remote(u, 0, at((1 - core) * 128, 128), r0.at[pool], core_peer)]
        if stage == 1:
            return [remote(u, 1, at(half + (1 - xpos) * 32, 32), r1.at[0, pool], x_peer),
                    remote(u, 2, at(half + 64 + (1 - ypos) * 32, 32), r1.at[1, pool], y_peer)]
        if stage == 2:
            return [remote(u, 3, at(a_half + (1 - ypos) * 16, 16), r2.at[0, pool], y_peer),
                    remote(u, 4, at(b_half + (1 - xpos) * 16, 16), r2.at[1, pool], x_peer)]
        if stage == 3:
            return [remote(u, 5, at(own_a, 16), at(own_a, 16), y_peer),
                    remote(u, 6, at(own_b, 16), at(own_b, 16), x_peer)]
        if stage == 4:
            return [remote(u, 7, at(a_half, 32), at(a_half, 32), x_peer),
                    remote(u, 8, at(b_half, 32), at(b_half, 32), y_peer)]
        return [remote(u, 9, at(half, 128), at(half, 128), core_peer)]

    slots = {0: [(0, core_peer)], 1: [(1, x_peer), (2, y_peer)], 2: [(3, y_peer), (4, x_peer)]}

    def start(u, stage):
        if stage >= 3:
            for slot, _ in slots[5 - stage]:
                pl.semaphore_wait(sent_sem.at[u, slot], 1)
        for copy in exchange(u, stage):
            copy.start()

    def finish(u, stage):
        for copy in exchange(u, stage):
            copy.wait()
        if stage < 3:
            for slot, peer in slots[stage]:
                pl.semaphore_signal(sent_sem.at[u, slot], inc=1, device_id=(peer,), device_id_type=MESH)

    def add_rows(u, row, count, buf, lead):
        b0, n, p0 = UNITS[u]
        ds = pl.ds(pl.multiple_of(row, 16), count)

        def body(k, carry):
            acc[b0 + k, ds, :] += buf[lead + (p0 + k,)]
            return carry

        lax.fori_loop(0, n, body, 0)

    def factor_update(u):
        b0, n, _ = UNITS[u]
        rho = rho_ref[0, 0]
        fresh = (1.0 - rho) * (1.0 / batch_total)
        for k in range(b0, b0 + n):
            if k not in KINDS:
                continue
            kind, m, b, i, j = KINDS[k]
            for p in range(2):
                ds = pl.ds(pl.multiple_of(own[p], 16), 16)
                if kind == "big":
                    old = big_old[m, b, i, p * 16:p * 16 + 16, j * 256:j * 256 + 256]
                else:
                    old = small_old[m, b, p * 16:p * 16 + 16, :]
                acc[k, ds, :] = rho * old + fresh * acc[k, ds, :]

    def wide_product(first, slot):
        ds = [pl.ds(pl.multiple_of(own[p], 16), 16) for p in range(2)]
        left = jnp.concatenate(
            [jnp.concatenate([acc[first + j, d, :] for d in ds], axis=0) for j in range(4)], axis=1)
        left = left * (1.0 / batch_total)
        for j in range(4):
            prod = nn(left, inv[slot, :, j * 256:j * 256 + 256], HIGHEST)
            for p in range(2):
                acc[first + j, ds[p], :] = prod[p * 16:p * 16 + 16, :]

    def post(u):
        b0, n, _ = UNITS[u]
        factor_update(u)
        for b in range(2):
            if b0 <= DU[b] < b0 + n:
                for copy in inv_copies(b):
                    copy.wait()
                wide_product(DU[b], 0)
                wide_product(DD[b], 1)
                if b == 1:
                    for copy in inv_copies(0):
                        copy.start()

    def out_copy(u):
        b0, n, _ = UNITS[u]
        return pltpu.make_async_copy(acc.at[pl.ds(b0, n)], out.at[pl.ds(b0, n)], out_sem.at[u])

    def advance(u, step):
        if step == 0:
            start(u, 0)
            return
        finish(u, step - 1)
        if step == 1:
            add_rows(u, half, 128, r0, ())
        elif step == 2:
            add_rows(u, a_half, 32, r1, (0,))
            add_rows(u, b_half, 32, r1, (1,))
        elif step == 3:
            add_rows(u, own_a, 16, r2, (0,))
            add_rows(u, own_b, 16, r2, (1,))
            post(u)
        if step < 6:
            start(u, step)
        else:
            out_copy(u).start()

    def ticks(i, plan):
        for t in sorted(set(t for t, _, _ in plan)):
            @pl.when(i == t)
            def _():
                for when, u, step in plan:
                    if when == t:
                        advance(u, step)

    def symmetric(base, ref):
        for i, j in UPPER:
            acc[base + upper_index(i, j)] += nt(ref[i * 256:i * 256 + 256, :], ref[j * 256:j * 256 + 256, :])

    def rectangle(base, left, ref):
        for j in range(4):
            acc[base + j] += nt(left, ref[j * 256:j * 256 + 256, :])

    def forward_tile(b, r, u_t):
        z = nn(wup_t[b, r * 256:r * 256 + 256, :], u_t).astype(BF16).astype(F32)
        sq, s = half_gelu(z)
        h_t[r * 256:r * 256 + 256, :] = (z * s).astype(BF16)
        return z, sq, s

    def backward_tile(b, r, q_t, parts):
        z, sq, s = parts
        dh = nn(wdn[b, r * 256:r * 256 + 256, :], q_t).astype(BF16).astype(F32)
        slope = s + (z * (s - s * s)) * (6 * C1 * sq + 2 * C0)
        g_t[r * 256:r * 256 + 256, :] = (dh * slope).astype(BF16)

    def tile_slice(i):
        return pl.ds(pl.multiple_of(i * TILE, TILE), TILE)

    def pass_one(i, carry):
        ds = tile_slice(i)
        tok_copy(i).wait()
        grad_copy(i).wait()
        u_t = tok[ds, :].T
        q_t = grad[ds, :].T
        for r in range(4):
            forward_tile(0, r, u_t)
        u1_t[:, ds] = nn(wdn_t[...], h_t[...]).astype(BF16)
        acc[AU0] += nt(u_t, u_t)
        acc[SD1] += nt(q_t, q_t)
        symmetric(AD0, h_t)
        return carry

    def pass_two(i, carry):
        ds = tile_slice(i)
        q_t = grad[ds, :].T
        u_t = u1_t[:, ds]
        for r in range(4):
            backward_tile(1, r, q_t, forward_tile(1, r, u_t))
        e1_t[:, ds] = nn(wup[1], g_t[...]).astype(BF16)
        acc[AU1] += nt(u_t, u_t)
        symmetric(AD1, h_t)
        rectangle(DD1, q_t, h_t)
        symmetric(SU1, g_t)
        rectangle(DU1, u_t, g_t)
        ticks(i, PLAN_TWO)
        return carry

    def pass_three(i, carry):
        ds = tile_slice(i)
        u_t = tok[ds, :].T
        e_t = e1_t[:, ds]
        for r in range(4):
            backward_tile(0, r, e_t, forward_tile(0, r, u_t))
        acc[SD0] += nt(e_t, e_t)
        rectangle(DD0, e_t, h_t)
        symmetric(SU0, g_t)
        rectangle(DU0, u_t, g_t)
        ticks(i, PLAN_THREE)
        return carry

    lax.fori_loop(0, tiles, pass_one, 0)
    for u in (0, 1):
        advance(u, 0)
    lax.fori_loop(0, tiles, pass_two, 0)
    for u in (2, 3, 4):
        advance(u, 0)
    lax.fori_loop(0, tiles, pass_three, 0)
    for u, step in TAIL:
        advance(u, step)
    for u in ALL:
        out_copy(u).wait()


PLAN_TWO = [(0, 0, 1), (0, 1, 1), (2, 0, 2), (3, 1, 2), (4, 0, 3), (5, 1, 3), (6, 0, 4), (7, 1, 4), (8, 0, 5), (9, 1, 5),
            (10, 0, 6), (11, 1, 6)]
PLAN_THREE = [(0, 2, 1), (0, 3, 1), (1, 4, 1), (3, 2, 2), (6, 3, 2), (8, 4, 2), (10, 2, 3), (11, 3, 3), (12, 4, 3),
              (14, 2, 4), (15, 3, 4)]
TAIL = [(4, 4), (2, 5), (3, 5), (4, 5), (2, 6), (3, 6), (6, 0), (5, 0), (6, 1), (5, 1), (4, 6), (6, 2), (5, 2), (6, 3), (5, 3),
        (6, 4), (5, 4), (6, 5), (5, 5), (6, 6), (5, 6)]


def assemble_kernel(g_hbm, a_up_inv, s_down_inv, p_up, p_down, a_up, s_up, a_down, s_down, g, sem):
    b = pl.program_id(0)
    i = pl.program_id(1)

    def copy_in(first, count, slot):
        return pltpu.make_async_copy(g_hbm.at[pl.ds(first, count)], g.at[pl.ds(first, count)], sem.at[slot])

    parts = []
    for layer in range(2):
        mine = []
        for first, count in ((AU[layer], 1), (SD[layer], 1), (DU[layer], 4), (DD[layer], 4), (AD[layer], 10), (SU[layer], 10)):
            mine.append(copy_in(first, count, len(parts) * 6 + len(mine)))
        parts.append(mine)

    @pl.when(jnp.logical_and(b == 0, i == 0))
    def _():
        for mine in parts:
            for copy in mine:
                copy.start()

    for layer in range(2):
        @pl.when(jnp.logical_and(b == layer, i == 0))
        def _():
            for copy in parts[layer]:
                copy.wait()

        for row in range(4):
            @pl.when(jnp.logical_and(b == layer, i == row))
            def _():
                r64 = slice(row * 64, row * 64 + 64)
                a_up[0] = g[AU[layer], r64, :]
                s_down[0] = g[SD[layer], r64, :]
                for j in range(4):
                    cols = slice(j * 256, j * 256 + 256)
                    p_up[0, :, cols] = nn(a_up_inv[0, r64, :], g[DU[layer] + j], HIGHEST)
                    for dst, base in ((a_down, AD[layer]), (s_up, SU[layer])):
                        if row <= j:
                            dst[0, :, cols] = g[base + upper_index(row, j)]
                        else:
                            dst[0, :, cols] = g[base + upper_index(j, row)].T
                p_down[0] = nn(g[DD[layer] + row].T, s_down_inv[0], HIGHEST)


def solution(mesh):
    shards = mesh.shape["data"]
    vmem = pltpu.VMEM
    whole = pl.BlockSpec(memory_space=vmem)
    anywhere = pl.BlockSpec(memory_space=pl.ANY)

    def local_step(tokens, out_grad, w_up, w_down, a_up_old, s_up_old, a_down_old, s_down_old,
                   a_up_inv, s_up_inv, a_down_inv, s_down_inv, factor_decay):
        rows = tokens.shape[0]
        tiles = rows // TILE
        dma = pltpu.SemaphoreType.DMA
        gathered = pl.pallas_call(
            functools.partial(main_kernel, rows, rows * shards),
            out_shape=jax.ShapeDtypeStruct((BLOCKS, 256, 256), F32),
            in_specs=[anywhere, anywhere, whole, whole, pl.BlockSpec(memory_space=pltpu.SMEM)] + [anywhere] * 6,
            out_specs=anywhere,
            scratch_shapes=[
                vmem((rows, D), BF16), vmem((rows, D), BF16),
                vmem((2, FF, D), BF16), vmem((D, FF), BF16),
                vmem((D, rows), BF16), vmem((D, rows), BF16),
                vmem((FF, TILE), BF16), vmem((FF, TILE), BF16),
                vmem((BLOCKS, 256, 256), F32),
                vmem((2, 2, 4, 32, FF), F32), vmem((2, 2, 32, D), F32), vmem((2, FF, FF), F32),
                vmem((POOL, 128, 256), F32), vmem((2, POOL, 32, 256), F32), vmem((2, POOL, 16, 256), F32),
                dma((tiles,)), dma((tiles,)), dma((2,)), dma((2,)), dma((len(UNITS),)),
                dma((len(UNITS), 10)), dma((len(UNITS), 10)),
                pltpu.SemaphoreType.REGULAR((len(UNITS), 5)),
            ],
            compiler_params=pltpu.CompilerParams(collective_id=0, has_side_effects=True,
                                                 vmem_limit_bytes=63 * 2 ** 20),
            name="passes_and_sums",
        )(tokens, out_grad, w_up, w_down, factor_decay.reshape(1, 1), a_up_old, s_up_old, a_down_old, s_down_old,
          s_up_inv, a_down_inv)

        def layer_rows(r, c):
            return pl.BlockSpec((1, r, c), lambda b, i: (b, i, 0))

        layer = pl.BlockSpec((1, D, D), lambda b, i: (b, 0, 0))
        shape = jax.ShapeDtypeStruct
        return tuple(pl.pallas_call(
            assemble_kernel,
            grid=(2, 4),
            out_shape=(shape((2, D, FF), F32), shape((2, FF, D), F32), shape((2, D, D), F32),
                       shape((2, FF, FF), F32), shape((2, FF, FF), F32), shape((2, D, D), F32)),
            in_specs=[anywhere, layer, layer],
            out_specs=(layer_rows(64, FF), layer_rows(256, D), layer_rows(64, D), layer_rows(256, FF),
                       layer_rows(256, FF), layer_rows(64, D)),
            scratch_shapes=[vmem((BLOCKS, 256, 256), F32), dma((12,))],
            compiler_params=pltpu.CompilerParams(vmem_limit_bytes=40 * 2 ** 20),
            name="write_outputs",
        )(gathered, a_up_inv, s_down_inv))

    batch_spec = P("data", None)
    replicated = P()
    return jax.shard_map(local_step, mesh=mesh, in_specs=(batch_spec, batch_spec) + (replicated,) * 11,
                         out_specs=(replicated,) * 6, check_vma=False)
```

time: 623 us -> 254 us (0.41); the launches traced: 614 us -> 254 us
  matrix products: 293 us -> 0 us
  waiting for transfers between devices: 264 us -> 0 us
  Pallas kernels: 0 us -> 252 us
  other arithmetic: 38.2 us -> 0 us
  between operations: 15.4 us -> 1.5 us
    dot_general x22 -> x0, matrix products: 293 us -> none  [the longest x12 168 us: cross_sum(): jnp.einsum('ti,tj->ij', left, right, preferred_element_type=jnp.float32)]
    psum x1 -> x0, waiting for transfers between devices: 264 us -> none  [local_step(): totals = [lax.psum(part, 'data') for part in local_parts]]
    pallas_call x0 -> x2, Pallas kernels: none -> 252 us  [the longest x1 237 us: local_step(): pl.pallas_call(functools.partial(main_kernel, rows, rows * shards), out_s...]
    add x2 -> x0, other arithmetic: 19.9 us -> none  [update_outputs(): factor_decay * old_part + (1.0 - factor_decay) * new_part]
    div x6 -> x0, other arithmetic: 18.3 us -> none  [stacked_sums(): jnp.stack([cross_sum(left, right) for left, right in zip(left_list, right...]
  transfers between devices with their start and end apart: 1 -> 0, of which waited for: 1 -> 0; matrix products, arithmetic and copies ran while one was open for 0% -> 0% of each run, Pallas kernels for 0% -> 0%
where the time goes in v1:
time: 254 us
  Pallas kernels  252 us (99%)
    pallas_call x1, Pallas kernels, local_step(): pl.pallas_call(functools.partial(main_kernel, rows, rows * shards), out_s...  237 us
    pallas_call x1, Pallas kernels, local_step(): pl.pallas_call(assemble_kernel, grid=(2, 4), out_shape=(shape((2, D, FF),...  14.8 us

profile of v1, /device:TPU:0, one launch (start us, length us, event | category | flops | bytes accessed | tf_op | source)
XLA Modules:
  0.0 254.1 jit_solution(2206063680867503868)
XLA Ops:
  1.3 0.0 copy-start
  1.3 236.8 %passes_and_sums.1.g_hbm = f32[60,256,256]{2,1,0:T(8,128)} custom-call(bf16[8192,256]{1,0:T(8,128)(2,1)} %tok_hbm.1, bf16[8192,256]{1,0:T(8,128)(2,1)} %grad_hbm.1, bf16[2,256,1024]{2,1,0:T(8,128)(2,1)} %wup.1, bf16[2,1024,256]{2,1,0:T(8,128)(2,1)} %wdn.1, f32[1,1]{1,0:T(1,128)} %bitcast.1.rho_ref, f32[2,256,256]{2,1,0:T(8,128)} %a_up_old.1, ...), custom_call_target="tpu_custom_call" | custom-call | tf_op jit(solution)/shard_map/passes_and_sums/pallas_call | solution.py:395
  238.1 0.0 copy-done
  238.1 0.0 copy-start.1
  238.1 1.0 copy-done.1
  239.2 14.8 %write_outputs.1 = (f32[2,256,1024]{2,1,0:T(8,128)}, f32[2,1024,256]{2,1,0:T(8,128)}, f32[2,256,256]{2,1,0:T(8,128)}, f32[2,1024,1024]{2,1,0:T(8,128)}, f32[2,10...) custom-call(f32[60,256,256]{2,1,0:T(8,128)} %passes_and_sums.1.g_hbm, f32[2,256,256]{2,1,0:T(8,128)S(1)} %copy-done, ...), custom_call_target="tpu_custom_call" | custom-call | tf_op jit(solution)/shard_map/write_outputs/pallas_call | solution.py:423
Async XLA Ops:
  1.3 236.8 %copy-start = (f32[2,256,256]{2,1,0:T(8,128)S(1)}, f32[2,256,256]{2,1,0:T(8,128)}, u32[]{:S(2)}) copy-start(f32[2,256,256]{2,1,0:T(8,128)} %a_up_inv.1) | copy-start | bytes 1572868
  238.1 1.0 copy-start.1

commit v2 on v1

v2 whole, which is shorter than its diff:
```python
import functools

import jax
import jax.numpy as jnp
from jax import lax
from jax.experimental import pallas as pl
from jax.experimental.pallas import tpu as pltpu
from jax.sharding import PartitionSpec as P

F32 = jnp.float32
BF16 = jnp.bfloat16
MESH = pl.DeviceIdType.MESH
HIGHEST = lax.Precision.HIGHEST

D = 256
FF = 1024
TILE = 1024
C0 = 0.7978845608028654
C1 = C0 * 0.044715

AU0, SD1, AD0, AU1, AD1, DD1, DU1, SU1, SD0, DU0, DD0, SU0 = 0, 1, 2, 11, 12, 21, 25, 29, 38, 39, 43, 47
BLOCKS = 56
AU = (AU0, AU1)
SD = (SD0, SD1)
AD = (AD0, AD1)
SU = (SU0, SU1)
DU = (DU0, DU1)
DD = (DD0, DD1)
ABOVE = ((0, 1), (0, 2), (1, 2), (0, 3), (1, 3), (2, 3))
LAST = ((0, 0), (0, 1), (1, 1))

UNITS = ((0, 5, 0), (5, 6, 5), (11, 7, 11), (18, 7, 18), (25, 4, 25), (29, 9, 29), (38, 9, 0), (47, 5, 11), (52, 4, 18))
POOL = 38

AFTER_1 = ((0, 0), (1, 0))
PLAN_2A = ((0, 0, 1), (0, 1, 1), (2, 0, 2), (3, 1, 2), (4, 0, 3), (5, 1, 3), (6, 0, 4), (7, 1, 4))
AFTER_2A = ((2, 0), (3, 0))
PLAN_2B = ((0, 0, 5), (0, 2, 1), (0, 3, 1), (1, 0, 6), (1, 1, 5), (2, 1, 6), (2, 2, 2), (4, 2, 3), (4, 3, 2), (6, 2, 4), (6, 3, 3))
AFTER_2B = ((4, 0),)
PLAN_2C = ((0, 2, 5), (1, 3, 4), (1, 4, 1), (2, 2, 6), (6, 3, 5), (7, 4, 2))
AFTER_2C = ((5, 0),)
PLAN_3A = ((0, 3, 6), (0, 4, 3), (0, 5, 1), (1, 4, 4), (3, 5, 2), (4, 4, 5), (5, 4, 6), (5, 5, 3), (7, 5, 4))
AFTER_3A = ((6, 0),)
PLAN_3B = ((2, 6, 1), (4, 5, 5), (7, 5, 6))
AFTER_3B = ((7, 0), (8, 0))
TAIL = ((6, 2), (7, 1), (8, 1), (6, 3), (7, 2), (8, 2), (6, 4), (7, 3), (8, 3), (6, 5), (7, 4), (8, 4), (6, 6), (7, 5), (7, 6), (8, 5), (8, 6))


def block_kinds():
    kinds = {}
    for b in range(2):
        for m, base in enumerate((AD[b], SU[b])):
            for k, (i, j) in enumerate(ABOVE):
                kinds[base + k] = ("above", m, b, i, j)
            for k in range(3):
                kinds[base + 6 + k] = ("diagonal", m, b, k, k)
        kinds[AU[b]] = ("small", 0, b, 0, 0)
        kinds[SD[b]] = ("small", 1, b, 0, 0)
    return kinds


KINDS = block_kinds()


def nn(a, b, precision=None):
    return lax.dot_general(a, b, (((1,), (0,)), ((), ())), preferred_element_type=F32, precision=precision)


def nt(a, b):
    return lax.dot_general(a, b, (((1,), (1,)), ((), ())), preferred_element_type=F32)


def half_gelu(z):
    sq = z * z
    return sq, jnp.tanh(z * (C1 * sq + C0)) * 0.5 + 0.5


def main_kernel(rows, batch_total,
                tok_hbm, grad_hbm, wup, wdn, rho_ref, a_up_old, s_up_old, a_down_old, s_down_old, s_up_inv, a_down_inv,
                acc, g_hbm, tok, grad, wup_t, wdn_t, u1_t, h_t, g_t, big_old, corner_old, small_old, inv,
                r0, r1, r2, tok_sem, grad_sem, old_sem, inv_sem, g_sem, send_sem, recv_sem, sent_sem):
    tiles = rows // TILE
    me = lax.axis_index("data")
    core = lax.rem(me, 2)
    xpos = lax.rem(me // 2, 2)
    ypos = me // 4
    core_peer = me + 1 - 2 * core
    x_peer = me + 2 - 4 * xpos
    y_peer = me + 4 - 8 * ypos

    barrier = pltpu.get_barrier_semaphore()
    for peer in (core_peer, x_peer, y_peer):
        pl.semaphore_signal(barrier, inc=1, device_id=(peer,), device_id_type=MESH)

    def tok_copy(i):
        ds = pl.ds(i * TILE, TILE)
        return pltpu.make_async_copy(tok_hbm.at[ds, :], tok.at[ds, :], tok_sem.at[i])

    def grad_copy(i):
        ds = pl.ds(i * TILE, TILE)
        return pltpu.make_async_copy(grad_hbm.at[ds, :], grad.at[ds, :], grad_sem.at[i])

    for i in range(tiles):
        tok_copy(i).start()
        grad_copy(i).start()

    half = core * 128
    a_half = half + xpos * 32
    b_half = half + 64 + ypos * 32
    own_a = a_half + ypos * 16
    own_b = b_half + xpos * 16
    own = (own_a, own_b)

    for m, old in enumerate((a_down_old, s_up_old)):
        for b in range(2):
            for i in range(3):
                for p in range(2):
                    dst = pl.ds(p * 16, 16)
                    pltpu.make_async_copy(old.at[b, pl.ds(i * 256 + own[p], 16), :],
                                          big_old.at[m, b, i, dst, :], old_sem.at[0]).start()
                    row = i * 256 + own[p] + core * (768 + 128 * LAST[i][0] - 128 - i * 256)
                    col = i * 256 + core * (768 + 128 * LAST[i][1] - i * 256)
                    pltpu.make_async_copy(old.at[b, pl.ds(pl.multiple_of(row, 16), 16), pl.ds(pl.multiple_of(col, 128), 128)],
                                          corner_old.at[m, b, i, dst, :], old_sem.at[2]).start()
    for m, old in enumerate((a_up_old, s_down_old)):
        for b in range(2):
            for p in range(2):
                pltpu.make_async_copy(old.at[b, pl.ds(own[p], 16), :],
                                      small_old.at[m, b, pl.ds(p * 16, 16), :], old_sem.at[1]).start()

    def inv_copy(slot, b):
        return pltpu.make_async_copy((s_up_inv, a_down_inv)[slot].at[b], inv.at[slot], inv_sem.at[slot])

    for slot in range(2):
        inv_copy(slot, 1).start()

    for b in range(2):
        wup_t[b] = wup[b].T
    wdn_t[...] = wdn[0].T
    acc[...] = jnp.zeros_like(acc)

    pltpu.make_async_copy(big_old, big_old, old_sem.at[0]).wait()
    pltpu.make_async_copy(small_old, small_old, old_sem.at[1]).wait()
    pltpu.make_async_copy(corner_old, corner_old, old_sem.at[2]).wait()
    pl.semaphore_wait(barrier, 3)

    def remote(u, slot, src, dst, peer):
        return pltpu.make_async_remote_copy(src_ref=src, dst_ref=dst, send_sem=send_sem.at[u, slot],
                                            recv_sem=recv_sem.at[u, slot], device_id=(peer,), device_id_type=MESH)

    def exchange(u, stage):
        b0, n, p0 = UNITS[u]
        blk = pl.ds(b0, n)
        pool = pl.ds(p0, n)

        def at(row, count):
            return acc.at[blk, pl.ds(pl.multiple_of(row, 16), count), :]

        if stage == 0:
            return [remote(u, 0, at((1 - core) * 128, 128), r0.at[pool], core_peer)]
        if stage == 1:
            return [remote(u, 1, at(half + (1 - xpos) * 32, 32), r1.at[0, pool], x_peer),
                    remote(u, 2, at(half + 64 + (1 - ypos) * 32, 32), r1.at[1, pool], y_peer)]
        if stage == 2:
            return [remote(u, 3, at(a_half + (1 - ypos) * 16, 16), r2.at[0, pool], y_peer),
                    remote(u, 4, at(b_half + (1 - xpos) * 16, 16), r2.at[1, pool], x_peer)]
        if stage == 3:
            return [remote(u, 5, at(own_a, 16), at(own_a, 16), y_peer),
                    remote(u, 6, at(own_b, 16), at(own_b, 16), x_peer)]
        if stage == 4:
            return [remote(u, 7, at(a_half, 32), at(a_half, 32), x_peer),
                    remote(u, 8, at(b_half, 32), at(b_half, 32), y_peer)]
        return [remote(u, 9, at(half, 128), at(half, 128), core_peer)]

    slots = {0: [(0, core_peer)], 1: [(1, x_peer), (2, y_peer)], 2: [(3, y_peer), (4, x_peer)]}

    def start(u, stage):
        if stage >= 3:
            for slot, _ in slots[5 - stage]:
                pl.semaphore_wait(sent_sem.at[u, slot], 1)
        for copy in exchange(u, stage):
            copy.start()

    def finish(u, stage):
        for copy in exchange(u, stage):
            copy.wait()
        if stage < 3:
            for slot, peer in slots[stage]:
                pl.semaphore_signal(sent_sem.at[u, slot], inc=1, device_id=(peer,), device_id_type=MESH)

    def add_rows(u, row, count, buf, lead):
        b0, n, p0 = UNITS[u]
        ds = pl.ds(pl.multiple_of(row, 16), count)

        def body(k, carry):
            acc[b0 + k, ds, :] += buf[lead + (p0 + k,)]
            return carry

        lax.fori_loop(0, n, body, 0)

    def factor_update(u):
        b0, n, _ = UNITS[u]
        rho = rho_ref[0, 0]
        fresh = (1.0 - rho) * (1.0 / batch_total)
        for k in range(b0, b0 + n):
            if k not in KINDS:
                continue
            kind, m, b, i, j = KINDS[k]
            for p in range(2):
                ds = pl.ds(pl.multiple_of(own[p], 16), 16)
                if kind == "small":
                    parts = [(slice(0, 256), small_old[m, b, p * 16:p * 16 + 16, :])]
                elif kind == "above":
                    parts = [(slice(0, 256), big_old[m, b, i, p * 16:p * 16 + 16, j * 256:j * 256 + 256])]
                else:
                    parts = [(slice(0, 128), corner_old[m, b, i, p * 16:p * 16 + 16, :]),
                             (slice(128, 256), big_old[m, b, i, p * 16:p * 16 + 16, i * 256 + 128:i * 256 + 256])]
                for cols, old in parts:
                    acc[k, ds, cols] = rho * old + fresh * acc[k, ds, cols]

    def wide_product(first, slot):
        ds = [pl.ds(pl.multiple_of(own[p], 16), 16) for p in range(2)]
        left = jnp.concatenate(
            [jnp.concatenate([acc[first + j, d, :] for d in ds], axis=0) for j in range(4)], axis=1)
        left = left * (1.0 / batch_total)
        for j in range(4):
            prod = nn(left, inv[slot, :, j * 256:j * 256 + 256], HIGHEST)
            for p in range(2):
                acc[first + j, ds[p], :] = prod[p * 16:p * 16 + 16, :]

    def post(u):
        b0, n, _ = UNITS[u]
        factor_update(u)
        for b in (1, 0):
            for slot, first in enumerate((DU[b], DD[b])):
                if b0 <= first < b0 + n:
                    inv_copy(slot, b).wait()
                    wide_product(first, slot)
                    if b == 1:
                        inv_copy(slot, 0).start()

    def advance(u, step):
        if step == 0:
            start(u, 0)
            return
        finish(u, step - 1)
        if step == 1:
            add_rows(u, half, 128, r0, ())
        elif step == 2:
            add_rows(u, a_half, 32, r1, (0,))
            add_rows(u, b_half, 32, r1, (1,))
        elif step == 3:
            add_rows(u, own_a, 16, r2, (0,))
            add_rows(u, own_b, 16, r2, (1,))
            post(u)
        if step < 6:
            start(u, step)

    def ticks(i, plan):
        for t in sorted(set(t for t, _, _ in plan)):
            @pl.when(i == t)
            def _():
                for when, u, step in plan:
                    if when == t:
                        advance(u, step)

    def symmetric(base, ref):
        def rows_of(i):
            return ref[i * 256:i * 256 + 256, :]

        for k, (i, j) in enumerate(ABOVE):
            acc[base + k] += nt(rows_of(i), rows_of(j))
        for k in range(3):
            prod = nt(rows_of(k), rows_of(k))
            acc[base + 6 + k, 0:128, :] += prod[0:128, :]
            acc[base + 6 + k, 128:256, 128:256] += prod[128:256, 128:256]
        prod = nt(rows_of(3), rows_of(3))
        for k, (i, j) in enumerate(LAST):
            acc[base + 6 + k, 128:256, 0:128] += prod[i * 128:i * 128 + 128, j * 128:j * 128 + 128]

    def rectangle(base, left, ref):
        for j in range(4):
            acc[base + j] += nt(left, ref[j * 256:j * 256 + 256, :])

    def half_tile(b, r, u_t):
        z = nn(wup_t[b, r * 256:r * 256 + 256, :], u_t).astype(BF16).astype(F32)
        return (z,) + half_gelu(z)

    def forward_tile(r, parts):
        z, _, s = parts
        h_t[r * 256:r * 256 + 256, :] = (z * s).astype(BF16)

    def backward_tile(b, r, q_t, g, parts):
        z, sq, s = parts
        dh = nn(wdn[b, r * 256:r * 256 + 256, :], q_t).astype(BF16).astype(F32)
        slope = s + (z * (s - s * s)) * (6 * C1 * sq + 2 * C0)
        g[r * 256:r * 256 + 256, :] = (dh * slope).astype(BF16)

    def tile_slice(i):
        return pl.ds(pl.multiple_of(i * TILE, TILE), TILE)

    def g_out(i, slot):
        return pltpu.make_async_copy(g_t.at[slot], g_hbm.at[i], g_sem.at[slot])

    def g_in(i, slot):
        return pltpu.make_async_copy(g_hbm.at[i], g_t.at[slot], g_sem.at[slot])

    def g_begin(i, slot):
        @pl.when(i >= 2)
        def _():
            g_out(i - 2, slot).wait()

    def g_end(i, slot):
        @pl.when(i < tiles - 2)
        def _():
            g_out(i, slot).start()

    def pass_1(i, carry):
        ds = tile_slice(i)
        tok_copy(i).wait()
        grad_copy(i).wait()
        u_t = tok[ds, :].T
        q_t = grad[ds, :].T
        for r in range(4):
            forward_tile(r, half_tile(0, r, u_t))
        u1_t[:, ds] = nn(wdn_t[...], h_t[...]).astype(BF16)
        acc[AU0] += nt(u_t, u_t)
        acc[SD1] += nt(q_t, q_t)
        symmetric(AD0, h_t)
        return carry

    def pass_2a(i, carry):
        ds = tile_slice(i)
        q_t = grad[ds, :].T
        u_t = u1_t[:, ds]
        for r in range(4):
            forward_tile(r, half_tile(1, r, u_t))
        acc[AU1] += nt(u_t, u_t)
        symmetric(AD1, h_t)
        rectangle(DD1, q_t, h_t)
        ticks(i, PLAN_2A)
        return carry

    def pass_2b(i, carry):
        ds = tile_slice(i)
        slot = lax.rem(i, 2)
        g = g_t.at[slot]
        q_t = grad[ds, :].T
        u_t = u1_t[:, ds]
        g_begin(i, slot)
        for r in range(4):
            backward_tile(1, r, q_t, g, half_tile(1, r, u_t))
        g_end(i, slot)
        rectangle(DU1, u_t, g)
        u1_t[:, ds] = nn(wup[1], g[...]).astype(BF16)
        ticks(i, PLAN_2B)
        return carry

    def pass_3a(i, carry):
        ds = tile_slice(i)
        slot = lax.rem(i, 2)
        g = g_t.at[slot]
        u_t = tok[ds, :].T
        e_t = u1_t[:, ds]
        g_begin(i, slot)
        for r in range(4):
            parts = half_tile(0, r, u_t)
            forward_tile(r, parts)
            backward_tile(0, r, e_t, g, parts)
        g_end(i, slot)
        acc[SD0] += nt(e_t, e_t)
        rectangle(DD0, e_t, h_t)
        rectangle(DU0, u_t, g)
        ticks(i, PLAN_3A)
        return carry

    def square_pass(base, plan):
        def body(i, carry):
            slot = lax.rem(i, 2)

            @pl.when(i >= 2)
            def _():
                g_in(i - 2, slot).wait()

            symmetric(base, g_t.at[slot])

            @pl.when(i < tiles - 2)
            def _():
                g_in(i, slot).start()

            ticks(i, plan)
            return carry

        lax.fori_loop(0, tiles, body, 0)

    def steps(plan):
        for u, step in plan:
            advance(u, step)

    lax.fori_loop(0, tiles, pass_1, 0)
    steps(AFTER_1)
    lax.fori_loop(0, tiles, pass_2a, 0)
    steps(AFTER_2A)
    lax.fori_loop(0, tiles, pass_2b, 0)
    steps(AFTER_2B)
    square_pass(SU1, PLAN_2C)
    steps(AFTER_2C)
    lax.fori_loop(0, tiles, pass_3a, 0)
    steps(AFTER_3A)
    square_pass(SU0, PLAN_3B)
    steps(AFTER_3B)
    steps(TAIL)


def symmetric_block(g, base, row, col):
    if row < col:
        return g[base + ABOVE.index((row, col))]
    if row > col:
        return g[base + ABOVE.index((col, row))].T
    if row < 3:
        top = g[base + 6 + row, 0:128, :]
        right = g[base + 6 + row, 128:256, 128:256]
    else:
        top = jnp.concatenate([g[base + 6, 128:256, 0:128], g[base + 7, 128:256, 0:128]], axis=1)
        right = g[base + 8, 128:256, 0:128]
    return jnp.concatenate([top, jnp.concatenate([top[:, 128:256].T, right], axis=1)], axis=0)


def assemble_kernel(g, a_up_inv, s_down_inv, p_up, p_down, a_up, s_up, a_down, s_down):
    b = pl.program_id(0)
    i = pl.program_id(1)
    for layer in range(2):
        for row in range(4):
            @pl.when(jnp.logical_and(b == layer, i == row))
            def _():
                for j in range(4):
                    cols = slice(j * 256, j * 256 + 256)
                    a_down[0, :, cols] = symmetric_block(g, AD[layer], row, j)
                    s_up[0, :, cols] = symmetric_block(g, SU[layer], row, j)
                if row == 0:
                    a_up[0] = g[AU[layer]]
                    s_down[0] = g[SD[layer]]
                for j in range(4):
                    cols = slice(j * 256, j * 256 + 256)
                    if row == 0:
                        p_up[0, :, cols] = nn(a_up_inv[0], g[DU[layer] + j], HIGHEST)
                    if row == 1:
                        p_down[0, cols, :] = nn(g[DD[layer] + j].T, s_down_inv[0], HIGHEST)


def solution(mesh):
    shards = mesh.shape["data"]
    vmem = pltpu.VMEM
    whole = pl.BlockSpec(memory_space=vmem)
    anywhere = pl.BlockSpec(memory_space=pl.ANY)

    def local_step(tokens, out_grad, w_up, w_down, a_up_old, s_up_old, a_down_old, s_down_old,
                   a_up_inv, s_up_inv, a_down_inv, s_down_inv, factor_decay):
        rows = tokens.shape[0]
        tiles = rows // TILE
        dma = pltpu.SemaphoreType.DMA
        sums, _ = pl.pallas_call(
            functools.partial(main_kernel, rows, rows * shards),
            out_shape=(vmem((BLOCKS, 256, 256), F32), jax.ShapeDtypeStruct((tiles, FF, TILE), BF16)),
            in_specs=[anywhere, anywhere, whole, whole, pl.BlockSpec(memory_space=pltpu.SMEM)] + [anywhere] * 6,
            out_specs=(whole, anywhere),
            scratch_shapes=[
                vmem((rows, D), BF16), vmem((rows, D), BF16),
                vmem((2, FF, D), BF16), vmem((D, FF), BF16),
                vmem((D, rows), BF16), vmem((FF, TILE), BF16), vmem((2, FF, TILE), BF16),
                vmem((2, 2, 3, 32, FF), F32), vmem((2, 2, 3, 32, 128), F32), vmem((2, 2, 32, D), F32), vmem((2, FF, FF), F32),
                vmem((POOL, 128, 256), F32), vmem((2, POOL, 32, 256), F32), vmem((2, POOL, 16, 256), F32),
                dma((tiles,)), dma((tiles,)), dma((3,)), dma((2,)), dma((2,)),
                dma((len(UNITS), 10)), dma((len(UNITS), 10)),
                pltpu.SemaphoreType.REGULAR((len(UNITS), 5)),
            ],
            compiler_params=pltpu.CompilerParams(collective_id=0, has_side_effects=True,
                                                 vmem_limit_bytes=48 * 2 ** 20),
            name="passes_and_sums",
        )(tokens, out_grad, w_up, w_down, factor_decay.reshape(1, 1), a_up_old, s_up_old, a_down_old, s_down_old,
          s_up_inv, a_down_inv)

        def layer_rows(r, c):
            return pl.BlockSpec((1, r, c), lambda b, i: (b, i, 0))

        def layer_whole(r, c):
            return pl.BlockSpec((1, r, c), lambda b, i: (b, 0, 0))

        shape = jax.ShapeDtypeStruct
        return tuple(pl.pallas_call(
            assemble_kernel,
            grid=(2, 4),
            out_shape=(shape((2, D, FF), F32), shape((2, FF, D), F32), shape((2, D, D), F32),
                       shape((2, FF, FF), F32), shape((2, FF, FF), F32), shape((2, D, D), F32)),
            in_specs=[whole, layer_whole(D, D), layer_whole(D, D)],
            out_specs=(layer_whole(D, FF), layer_whole(FF, D), layer_whole(D, D), layer_rows(256, FF),
                       layer_rows(256, FF), layer_whole(D, D)),
            compiler_params=pltpu.CompilerParams(vmem_limit_bytes=24 * 2 ** 20),
            name="write_outputs",
        )(sums, a_up_inv, s_down_inv))

    batch_spec = P("data", None)
    replicated = P()
    return jax.shard_map(local_step, mesh=mesh, in_specs=(batch_spec, batch_spec) + (replicated,) * 11,
                         out_specs=(replicated,) * 6, check_vma=False)
```

time: 254 us -> 227 us (0.89)
  Pallas kernels: 252 us -> 225 us
    pallas_call x1, Pallas kernels: 237 us -> 214 us  [local_step(): pl.pallas_call(functools.partial(main_kernel, rows, rows * shards), out_s...]
    pallas_call x1, Pallas kernels: 14.8 us -> 11.5 us  [local_step(): pl.pallas_call(assemble_kernel, grid=(2, 4), out_shape=(shape((2, D, FF),...]
where the time goes in v2:
time: 227 us
  Pallas kernels  225 us (99%)
    pallas_call x1, Pallas kernels, local_step(): pl.pallas_call(functools.partial(main_kernel, rows, rows * shards), out_s...  214 us
    pallas_call x1, Pallas kernels, local_step(): pl.pallas_call(assemble_kernel, grid=(2, 4), out_shape=(shape((2, D, FF),...  11.5 us

profile of v2, /device:TPU:0, one launch (start us, length us, event | category | flops | bytes accessed | tf_op | source)
XLA Modules:
  0.0 226.7 jit_solution(5122026703472115005)
XLA Ops:
  1.3 0.0 copy-start
  1.3 0.0 copy-start.1
  1.3 213.9 %passes_and_sums.1 = (f32[56,256,256]{2,1,0:T(8,128)S(1)}, bf16[8,1024,1024]{2,1,0:T(8,128)(2,1)}) custom-call(bf16[8192,256]{1,0:T(8,128)(2,1)} %tok_hbm.1, bf16[8192,256]{1,0:T(8,128)(2,1)} %grad_hbm.1, bf16[2,256,1024]{2,1,0:T(8,128)(2,1)} %wup.1, bf16[2,1024,256]{2,1,0:T(8,128)(2,1)} %wdn.1, f32[1,1]{1,0:T(1,128)} %bitcast.1.rho_ref, ...), custom_call_target="tpu_custom_call" | custom-call | tf_op jit(solution)/shard_map/passes_and_sums/pallas_call | solution.py:462
  215.2 0.0 copy-done
  215.2 0.0 copy-done.1
  215.2 11.5 %write_outputs.1 = (f32[2,256,1024]{2,1,0:T(8,128)}, f32[2,1024,256]{2,1,0:T(8,128)}, f32[2,256,256]{2,1,0:T(8,128)}, f32[2,1024,1024]{2,1,0:T(8,128)}, f32[2,10...) custom-call(f32[56,256,256]{2,1,0:T(8,128)S(1)} %get-tuple-element.7.g, f32[2,256,256]{2,1,0:T(8,128)S(1)} %copy-done, ...), custom_call_target="tpu_custom_call" | custom-call | tf_op jit(solution)/shard_map/write_outputs/pallas_call | solution.py:490
Async XLA Ops:
  1.3 213.9 %copy-start = (f32[2,256,256]{2,1,0:T(8,128)S(1)}, f32[2,256,256]{2,1,0:T(8,128)}, u32[]{:S(2)}) copy-start(f32[2,256,256]{2,1,0:T(8,128)} %a_up_inv.1) | copy-start | bytes 1572868
  1.3 213.9 %copy-start.1 = (f32[2,256,256]{2,1,0:T(8,128)S(1)}, f32[2,256,256]{2,1,0:T(8,128)}, u32[]{:S(2)}) copy-start(f32[2,256,256]{2,1,0:T(8,128)} %s_down_inv.1) | copy-start | bytes 1572868
